TPU v7x, 32 devices: a whole 2x2x4 slice. The times are simulated.
32 devices in a mesh: stn: 4 (over z), chan: 4 (over y, core), tile: 2 (over x).
Axes of the slice: x: 2, y: 2, z: 4, core: 2. Of those that a mesh axis runs over, the one named last changes fastest.
Arguments:
- model_image: bfloat16 [8, 64, 2048], P('tile', 'stn'), may hold values from -0.005859375 to 0.005859375
- station_beams: float32 [2, 64, 1024], replicated, may hold values from -6 to 6
- subgrid_offsets: int32 [4, 128, 2], P('chan'), may hold values from -4096 to 4064
- subgrid_stations: int32 [128, 2], P(('stn', 'tile')), may hold values from 0 to 63, as said below
- visibility_uv: float32 [2, 128, 512], P(None, ('stn', 'tile'), 'chan'), may hold values from 2 to 30
- observed: float32 [2, 32, 4, 512], P(None, ('stn', 'tile'), 'chan'), may hold values from -3 to 3
- live_counts: int32 [32, 4], P(('stn', 'tile'), 'chan'), may hold values from 1 to 8
Outputs:
- residual: float32 [2, 32, 4, 512], P(None, ('stn', 'tile'), 'chan')
Inputs may be any that keep to these rules, and one draw needn't show every extreme that they name: `subgrid_stations`: each row names two different stations. `live_counts`: rows with a time step at or beyond the count carry no data.
All inputs are finite; a program needn't handle non-finite values.
Results may differ from a plain program's by a relative error of at most 0.00071.
Values may be sent and summed in bfloat16 or wider, within the bound.
A program may use at most 64 MiB of HBM per device.

v0:
```python
import math
import jax
import jax.numpy as jnp
from jax import lax
from jax.sharding import PartitionSpec as P

SG = 32
NG = 8192
TIMES = 8
TILE_DEV = 4
TL = 64
SUB_TILE = 16
two_pi = 6.283185307179586


def phase_pair(products, modulus):
    angle_turns = jnp.mod(products, modulus).astype(jnp.float32) * (two_pi / modulus)
    return (jnp.cos(angle_turns), -jnp.sin(angle_turns))


def narrow_mix(pattern, left, right):
    return jnp.einsum(pattern, left, right, preferred_element_type=jnp.float32)


def exact_mix(pattern, left, right):
    return jnp.einsum(pattern, left, right, precision=lax.Precision.HIGHEST)


def tile_cuts(strip_rows, row_ids, offset_block, strip_half):
    block_size = offset_block.shape[0]
    columns = strip_rows.shape[1]
    pixel_idx = jnp.arange(SG, dtype=jnp.int32)
    col_pos = jnp.arange(columns, dtype=jnp.int32) - columns // 2
    v_index = offset_block[:, 1][:, None] + pixel_idx[None, :]
    ev_real, ev_imag = phase_pair(col_pos[:, None, None] * v_index[None, :, :], NG)
    phase_table = (
        jnp.stack([ev_real, ev_imag], axis=1)
        .reshape(columns, 2 * block_size * SG)
        .astype(jnp.bfloat16)
    )
    partial_q = jnp.dot(strip_rows, phase_table, preferred_element_type=jnp.float32).astype(
        jnp.bfloat16
    )
    partial_q = partial_q.reshape(strip_rows.shape[0], 2, block_size, SG)
    q_real = partial_q[:, 0]
    q_imag = partial_q[:, 1]
    u_index = offset_block[:, 0][:, None] + pixel_idx[None, :]
    row_pos = row_ids - strip_half
    eu_real, eu_imag = phase_pair(u_index[:, :, None] * row_pos[None, None, :], NG)
    eu_real = eu_real.astype(jnp.bfloat16)
    eu_imag = eu_imag.astype(jnp.bfloat16)
    cut_real = narrow_mix("jal,ljb->jab", eu_real, q_real) - narrow_mix(
        "jal,ljb->jab", eu_imag, q_imag
    )
    cut_imag = narrow_mix("jal,ljb->jab", eu_real, q_imag) + narrow_mix(
        "jal,ljb->jab", eu_imag, q_real
    )
    return jnp.stack([cut_real, cut_imag], axis=1).reshape(block_size, 2 * SG * SG)


def cuts_blocked(strip_rows, row_ids, offsets, strip_half):
    how_many = offsets.shape[0]
    block_size = math.gcd(how_many, 32)
    grouped = offsets.reshape(how_many // block_size, block_size, 2)
    stacked = lax.map(
        lambda offset_block: tile_cuts(strip_rows, row_ids, offset_block, strip_half), grouped
    )
    return stacked.reshape(how_many, 2 * SG * SG)


def predict(cut_rows, pair_ids, station_beams, uv_block):
    how_many = cut_rows.shape[0]
    cut_grid = cut_rows.reshape(how_many, 2, SG, SG)
    pixel_idx = jnp.arange(SG, dtype=jnp.int32)
    w_real, w_neg = phase_pair(pixel_idx[:, None] * pixel_idx[None, :], SG)
    w_imag = -w_neg
    c_real = cut_grid[:, 0]
    c_imag = cut_grid[:, 1]
    half_real = exact_mix("xa,jab->jxb", w_real, c_real) - exact_mix("xa,jab->jxb", w_imag, c_imag)
    half_imag = exact_mix("xa,jab->jxb", w_real, c_imag) + exact_mix("xa,jab->jxb", w_imag, c_real)
    sub_real = (
        exact_mix("jxb,yb->jxy", half_real, w_real) - exact_mix("jxb,yb->jxy", half_imag, w_imag)
    ) / (SG * SG)
    sub_imag = (
        exact_mix("jxb,yb->jxy", half_real, w_imag) + exact_mix("jxb,yb->jxy", half_imag, w_real)
    ) / (SG * SG)
    pixel_pos = pixel_idx.astype(jnp.float32)
    taper_line = 1.0 - ((2.0 * pixel_pos - (SG - 1)) / SG) ** 2
    taper_grid = (taper_line[:, None] * taper_line[None, :]).reshape(SG * SG)
    beam_first = station_beams[:, pair_ids[:, 0]]
    beam_second = station_beams[:, pair_ids[:, 1]]
    gain_real = (beam_first[0] * beam_second[0] + beam_first[1] * beam_second[1]) * taper_grid
    gain_imag = (beam_first[1] * beam_second[0] - beam_first[0] * beam_second[1]) * taper_grid
    flat_real = sub_real.reshape(how_many, SG * SG)
    flat_imag = sub_imag.reshape(how_many, SG * SG)
    weighted_real = (flat_real * gain_real - flat_imag * gain_imag).reshape(how_many, SG, SG)
    weighted_imag = (flat_real * gain_imag + flat_imag * gain_real).reshape(how_many, SG, SG)
    u_angle = uv_block[0][:, :, None] * pixel_pos[None, None, :] * (two_pi / SG)
    v_angle = uv_block[1][:, :, None] * pixel_pos[None, None, :] * (two_pi / SG)
    eu_real = jnp.cos(u_angle)
    eu_imag = -jnp.sin(u_angle)
    ev_real = jnp.cos(v_angle)
    ev_imag = -jnp.sin(v_angle)
    inner_real = exact_mix("jxy,jky->jxk", weighted_real, ev_real) - exact_mix(
        "jxy,jky->jxk", weighted_imag, ev_imag
    )
    inner_imag = exact_mix("jxy,jky->jxk", weighted_real, ev_imag) + exact_mix(
        "jxy,jky->jxk", weighted_imag, ev_real
    )
    vis_real = exact_mix("jkx,jxk->jk", eu_real, inner_real) - exact_mix(
        "jkx,jxk->jk", eu_imag, inner_imag
    )
    vis_imag = exact_mix("jkx,jxk->jk", eu_real, inner_imag) + exact_mix(
        "jkx,jxk->jk", eu_imag, inner_real
    )
    return jnp.stack([vis_real, vis_imag], axis=0)


def on_device(
    model_image,
    station_beams,
    subgrid_offsets,
    subgrid_stations,
    visibility_uv,
    observed,
    live_counts,
):
    tile_count = lax.axis_size("tile")
    columns = model_image.shape[2]
    strip_half = TILE_DEV * tile_count * TL // 2
    group_offsets = subgrid_offsets[0]
    stn_index = lax.axis_index("stn")
    tile_first = lax.axis_index("tile") * TILE_DEV
    tile_ids = jnp.arange(TILE_DEV, dtype=jnp.int32)
    group_size = SUB_TILE * tile_count
    station_offsets = lax.dynamic_slice_in_dim(group_offsets, stn_index * group_size, group_size, 0)
    shard_piece = lax.all_gather(model_image, "stn", axis=1, tiled=True)
    piece_rows = shard_piece.shape[1]
    piece_ids = (
        (tile_first + tile_ids)[:, None] * TL + jnp.arange(piece_rows, dtype=jnp.int32)[None, :]
    ).reshape(-1)
    piece_strip = shard_piece.reshape(TILE_DEV * piece_rows, columns)
    group_cuts = cuts_blocked(piece_strip, piece_ids, station_offsets, strip_half)
    own_cuts = lax.psum_scatter(group_cuts, "tile", scatter_dimension=0, tiled=True)
    predicted = predict(own_cuts, subgrid_stations, station_beams, visibility_uv)
    chan_count = lax.axis_size("chan")
    outgoing = predicted.reshape(2, SUB_TILE // chan_count, chan_count, predicted.shape[2])
    regrouped = lax.all_to_all(outgoing, "chan", split_axis=2, concat_axis=3, tiled=True)
    total_rows = regrouped.shape[3]
    time_step = jnp.mod(jnp.arange(total_rows, dtype=jnp.int32), TIMES)
    live_mask = time_step[None, None, :] < live_counts[:, :, None]
    return jnp.where(live_mask[None], observed - regrouped, 0.0)


def solution(mesh):
    return jax.shard_map(
        on_device,
        mesh=mesh,
        in_specs=(
            P("tile", "stn", None),
            P(),
            P("chan", None, None),
            P(("stn", "tile"), None),
            P(None, ("stn", "tile"), "chan"),
            P(None, ("stn", "tile"), "chan", None),
            P(("stn", "tile"), "chan"),
        ),
        out_specs=P(None, ("stn", "tile"), "chan", None),
        check_vma=False,
    )
```

profile of v0, /device:TPU:0, one launch (start us, length us, event | category | flops | bytes accessed | tf_op | source)
XLA Modules:
  0.0 118.8 jit_solution(3581766435553474679)
XLA Ops:
  6.5 0.0 copy-start
  6.5 0.0 all-gather.2.cloned.1.call-start
  6.5 0.7 all-gather.2.cloned.1.call-update
  7.3 0.0 reduce-scatter.2.cloned.1.call-start
  7.3 0.8 dynamic-slice_bitcast_fusion
  8.1 0.1 iota_add_fusion
  8.2 0.1 iota_add_fusion.1
  8.2 0.1 add_add_fusion
  8.3 0.8 fusion.66
  9.1 0.0 copy-done
  9.1 0.7 gather_fusion
  9.9 0.7 gather_fusion.1
  10.6 0.1 sub.67
  10.7 0.1 add.237
  10.8 0.1 sub.77
  11.0 35.5 %cosine_convert_fusion = (bf16[2048,1,32,32]{0,3,2,1:T(8,128)(2,1)S(1)}, bf16[2048,1,32,32]{0,3,2,1:T(8,128)(2,1)}) fusion(s32[32,32]{1,0:T(8,128)S(1)} %iota_add_fusion, s32[2048]{0:T(1024)S(1)} %iota_add_fusion.2), kind=kLoop, calls=%fused_computation.12 | loop fusion | flops 35651584 | bytes 8400896 | tf_op jit(solution)/shard_map/convert
  46.4 6.2 %pad_maximum_fusion = bf16[2048,2,32,32]{0,3,2,1:T(8,128)(2,1)} fusion(bf16[2048,1,32,32]{0,3,2,1:T(8,128)(2,1)} %get-tuple-element.31, bf16[2048,1,32,32]{0,3,2,1:T(8,128)(2,1)S(1)} %get-tuple-element.30), kind=kLoop, calls=%fused_computation.10 | loop fusion | flops 4194304 | bytes 16777216 | tf_op jit(solution)/shard_map/while/body/eval_jaxpr/stack | solution.py:37
  52.6 6.0 %convolution_convert_fusion = bf16[2048,256]{1,0:T(8,128)(2,1)S(1)} fusion(bf16[2048,2048]{0,1:T(8,128)(2,1)} %bitcast.90, bf16[256,2048]{1,0:T(8,128)(2,1)} %bitcast.96), kind=kOutput, calls=%fused_computation.13 | convolution fusion | flops 2148007936 | bytes 10485760 | tf_op jit(solution)/shard_map/while/body/eval_jaxpr/dot_general | solution.py:41
  58.6 4.0 %fusion.15 = f32[32,32,32]{2,1,0:T(8,128)S(1)} fusion(s32[256]{0:T(256)S(1)} %sub.67, s32[32,32]{1,0:T(8,128)S(1)} %iota_add_fusion.1, bf16[256,2,32,32]{0,3,2,1:T(8,128)(2,1)S(1)} %bitcast.97), kind=kOutput, calls=%fused_computation.44 | convolution fusion | flops 20709376 | bytes 672768 | tf_op jit(solution)/shard_map/while/body/eval_jaxpr/jal,ljb->jab/dot_general | solution.py:22
  62.6 4.0 %fusion.14 = f32[32,32,32]{2,1,0:T(8,128)S(1)} fusion(s32[256]{0:T(256)S(1)} %sub.67, s32[32,32]{1,0:T(8,128)S(1)} %iota_add_fusion.1, bf16[256,2,32,32]{0,3,2,1:T(8,128)(2,1)S(1)} %bitcast.98), kind=kOutput, calls=%fused_computation.43 | convolution fusion | flops 20709376 | bytes 672768 | tf_op jit(solution)/shard_map/while/body/eval_jaxpr/jal,ljb->jab/dot_general | solution.py:22
  66.6 4.3 %fusion.4 = f32[32,1,32,32]{3,2,0,1:T(8,128)S(1)} fusion(f32[32,32,32]{2,1,0:T(8,128)S(1)} %fusion.15, s32[256]{0:T(256)S(1)} %sub.67, s32[32,32]{1,0:T(8,128)S(1)} %iota_add_fusion.1, bf16[256,2,32,32]{0,3,2,1:T(8,128)(2,1)S(1)} %bitcast.99), kind=kOutput, calls=%fused_computation.22 | convolution fusion | flops 21004288 | bytes 1197056 | tf_op jit(solution)/shard_map/while/body/eval_jaxpr/jal,ljb->jab/dot_general | solution.py:22
  70.9 4.1 %fusion.3 = f32[32,1,32,32]{3,2,0,1:T(8,128)S(1)} fusion(f32[32,32,32]{2,1,0:T(8,128)S(1)} %fusion.14, s32[256]{0:T(256)S(1)} %sub.67, s32[32,32]{1,0:T(8,128)S(1)} %iota_add_fusion.1, bf16[256,2,32,32]{0,3,2,1:T(8,128)(2,1)S(1)} %bitcast.100), kind=kOutput, calls=%fused_computation.20 | convolution fusion | flops 21004288 | bytes 1197056 | tf_op jit(solution)/shard_map/while/body/eval_jaxpr/jal,ljb->jab/dot_general | solution.py:22
  75.0 0.1 pad_maximum_fusion.1
  75.1 0.1 copy.26
  75.2 1.2 %reshape.278 = f32[32,2048]{1,0:T(8,128)} reshape(f32[32,2,32,32]{3,2,1,0:T(8,128)S(1)} %copy.26) | data formatting | bytes 524288 | tf_op jit(solution)/shard_map/reshape | solution.py:68
  76.4 0.0 reduce-scatter.2.cloned.1.call-update
  76.4 0.1 broadcast_multiply_fusion
  76.5 0.0 copy-done.2
  76.5 14.6 %reduce-scatter.2.cloned.1.call-done = f32[16,2048]{1,0:T(8,128)} async-done(((f32[32,2048]{1,0:T(8,128)}), f32[16,2048]{1,0:T(8,128)}) %reduce-scatter.2.cloned.1.call-update) | async-done | bytes 131088 | tf_op jit(solution)/shard_map/reduce_scatter | solution.py:144
  91.1 1.1 reshape.279
  92.2 0.6 fusion.23
  92.8 0.6 fusion.22
  93.4 0.6 fusion.10
  94.0 0.6 fusion.46
  94.6 0.6 fusion.39
  95.2 0.6 fusion.9
  95.8 0.9 fusion.8
  96.6 0.6 multiply_add_fusion
  97.2 1.3 %fusion.18 = f32[16,32,128]{2,1,0:T(8,128)S(1)} fusion(f32[16,32,32]{2,1,0:T(8,128)S(1)} %get-tuple-element.27, f32[16,128]{1,0:T(8,128)S(1)} %get-tuple-element.33, f32[32]{0:T(128)S(1)} %iota_convert_fusion), kind=kOutput, calls=%fused_computation.56 | convolution fusion | flops 25296896 | bytes 336000 | tf_op jit(solution)/shard_map/jxy,jky->jxk/dot_general | solution.py:26
  98.6 1.3 %fusion.20 = f32[16,32,128]{2,1,0:T(8,128)S(1)} fusion(f32[16,32,32]{2,1,0:T(8,128)S(1)} %get-tuple-element.27, f32[16,128]{1,0:T(8,128)S(1)} %get-tuple-element.33, f32[32]{0:T(128)S(1)} %iota_convert_fusion), kind=kOutput, calls=%fused_computation.57 | convolution fusion | flops 25362432 | bytes 336000 | tf_op jit(solution)/shard_map/jxy,jky->jxk/dot_general | solution.py:26
  99.9 1.3 %fusion.6 = f32[16,128,32]{1,2,0:T(8,128)S(1)} fusion(f32[16,32,128]{2,1,0:T(8,128)S(1)} %fusion.18, f32[16,32,32]{2,1,0:T(8,128)S(1)} %get-tuple-element.26, f32[16,128]{1,0:T(8,128)S(1)} %get-tuple-element.33, f32[32]{0:T(128)S(1)} %iota_convert_fusion), kind=kOutput, calls=%fused_computation.26 | convolution fusion | flops 25427968 | bytes 598144 | tf_op jit(solution)/shard_map/jxy,jky->jxk/dot_general | solution.py:26
  101.2 2.4 %multiply_reduce_fusion.2 = (f32[16,128]{1,0:T(8,128)S(1)}, f32[16,128]{1,0:T(8,128)S(1)}, f32[16,128]{1,0:T(8,128)S(1)}, f32[16,128]{1,0:T(8,128)S(1)}) fusion(f32[32]{0:T(128)S(1)} %iota_convert_fusion, f32[16,128]{1,0:T(8,128)S(1)} %get-tuple-element.32, f32[16,128,32]{1,2,0:T(8,128)S(1)} %fusion.6, f32[16,32,128]{2,1,0:T(8,128)S(1)} %fusion.20, ...), kind=kOutput, calls=%fused_computation.49 | convolution fusion | flops 26075136 | bytes 639104 | tf_op jit(solution)/shard_map/jxy,jky->jxk/dot_general | solution.py:26
  103.6 0.6 copy.33
  104.2 3.3 %all-to-all-start = ((f32[2,4,4,128]{3,1,0,2:T(4,128)}), f32[2,4,4,128]{3,1,0,2:T(4,128)S(1)}, u32[]{:S(2)}, u32[]{:S(2)}) async-start(f32[2,4,4,128]{3,1,0,2:T(4,128)} %copy.33), calls=%async_computation.1 | async-start | bytes 32768 | tf_op jit(solution)/shard_map/all_to_all | solution.py:148
  107.5 0.0 copy-done.3
  107.5 0.1 broadcast_compare_fusion
  107.6 3.7 %all-to-all-done = f32[2,4,4,128]{3,1,0,2:T(4,128)S(1)} async-done(((f32[2,4,4,128]{3,1,0,2:T(4,128)}), f32[2,4,4,128]{3,1,0,2:T(4,128)S(1)}, u32[]{:S(2)}, u32[]{:S(2)}) %all-to-all-start) | async-done | bytes 16416 | tf_op jit(solution)/shard_map/all_to_all | solution.py:148
  111.4 0.6 copy.36
  (20 shorter events, 0.1 us)
Async XLA Ops:
  6.5 2.6 %copy-start = (f32[2,64,1024]{2,1,0:T(8,128)S(1)}, f32[2,64,1024]{2,1,0:T(8,128)}, u32[]{:S(2)}) copy-start(f32[2,64,1024]{2,1,0:T(8,128)} %param.8) | copy-start | bytes 1572868
  6.5 46.1 %all-gather.2.cloned.1.call-start = ((), (), s32[]{:S(2)}) async-start(), calls=%async_computation.2 | async-start | bytes 1310720 | tf_op jit(solution)/shard_map/all_gather | solution.py:137
  7.3 83.8 %reduce-scatter.2.cloned.1.call-start = ((), (), s32[]{:S(2)}) async-start(), calls=%async_computation.3 | async-start | bytes 393216 | tf_op jit(solution)/shard_map/reduce_scatter | solution.py:144
  66.6 9.9 %copy-start.2 = (f32[2,16,128]{2,1,0:T(8,128)S(1)}, f32[2,16,128]{2,1,0:T(8,128)}, u32[]{:S(2)}) copy-start(f32[2,16,128]{2,1,0:T(8,128)} %param.11) | copy-start | bytes 49156
  75.0 32.5 %copy-start.3 = (s32[4,1]{0,1:T(1,128)S(1)}, s32[4,1]{0,1:T(1,128)}, u32[]{:S(2)}) copy-start(s32[4,1]{0,1:T(1,128)} %param.13) | copy-start | bytes 52
  75.0 36.3 %copy-start.1 = (f32[2,4,1,512]{3,2,1,0:T(1,128)S(1)}, f32[2,4,1,512]{3,2,1,0:T(1,128)}, u32[]{:S(2)}) copy-start(f32[2,4,1,512]{3,2,1,0:T(1,128)} %param.12) | copy-start | bytes 49156
  104.2 7.1 %all-to-all-start = ((f32[2,4,4,128]{3,1,0,2:T(4,128)}), f32[2,4,4,128]{3,1,0,2:T(4,128)S(1)}, u32[]{:S(2)}, u32[]{:S(2)}) async-start(f32[2,4,4,128]{3,1,0,2:T(4,128)} %copy.33), calls=%async_computation.1 | async-start | bytes 32768 | tf_op jit(solution)/shard_map/all_to_all | solution.py:148
Sparse Core Ops, SparseCore 0:
  8.9 30.7 all-gather.1
  76.6 14.4 reduce-scatter.1
where the time goes:
time: 119 us
  other arithmetic  43 us (36%)
  matrix products  33.7 us (28%)
  waiting for transfers between devices  19 us (16%)
  between operations  13.6 us (11%)
  local copies, waits for them, and re-layouts  6.18 us (5%)
  starting transfers between devices  3.3 us (3%)
    another operation x1, other arithmetic  35.5 us
    dot_general x4, matrix products, narrow_mix(): return jnp.einsum(pattern, left, right, preferred_element_type=jnp.float32)  16.4 us
    reduce_scatter x1, waiting for transfers between devices, on_device(): lax.psum_scatter(group_cuts, 'tile', scatter_dimension=0, tiled=True)  14.6 us
    dot_general x12, matrix products, exact_mix(): return jnp.einsum(pattern, left, right, precision=lax.Precision.HIGHEST)  11.3 us
    another operation x1, other arithmetic, tile_cuts(): jnp.stack([ev_real, ev_imag], axis=1).reshape(columns, 2 * block_size * SG)  6.18 us
    dot_general x1, matrix products, tile_cuts(): jnp.dot(strip_rows, phase_table, preferred_element_type=jnp.float32)  6 us
    all_to_all x1, waiting for transfers between devices, on_device(): lax.all_to_all(outgoing, 'chan', split_axis=2, concat_axis=3, tiled=True)  3.74 us
    all_to_all x1, starting transfers between devices, on_device(): lax.all_to_all(outgoing, 'chan', split_axis=2, concat_axis=3, tiled=True)  3.25 us
  transfers between devices with their start and end apart: 3, of which 2 were waited for; matrix products, arithmetic and copies ran while one was open for 38% of the time, Pallas kernels for 0%

commit v1 on v0

--- a/solution.py
+++ b/solution.py
@@ -11,6 +11,17 @@
 TL = 64
 SUB_TILE = 16
 two_pi = 6.283185307179586
+
+
+def cut_along(array, dim, size):
+    before, after = (array.shape[:dim], array.shape[dim + 1 :])
+    return jnp.moveaxis(array.reshape(*before, size, -1, *after), dim, 0)
+
+
+def joined_along(blocks, dim):
+    shape = list(blocks.shape[1:])
+    shape[dim] *= blocks.shape[0]
+    return jnp.moveaxis(blocks, 0, dim).reshape(shape)
 
 
 def phase_pair(products, modulus):
@@ -145,7 +156,14 @@
     predicted = predict(own_cuts, subgrid_stations, station_beams, visibility_uv)
     chan_count = lax.axis_size("chan")
     outgoing = predicted.reshape(2, SUB_TILE // chan_count, chan_count, predicted.shape[2])
-    regrouped = lax.all_to_all(outgoing, "chan", split_axis=2, concat_axis=3, tiled=True)
+    size, here = (lax.axis_size("chan"), lax.axis_index("chan"))
+    parts = cut_along(outgoing, 2, size)
+    outs = [parts[here]]
+    for hop in range(1, size):
+        sent = parts[(here + hop) % size]
+        outs.append(lax.ppermute(sent, "chan", [(i, (i + hop) % size) for i in range(size)]))
+    parts = jnp.stack(outs)[(here - jnp.arange(size)) % size]
+    regrouped = joined_along(parts, 3)
     total_rows = regrouped.shape[3]
     time_step = jnp.mod(jnp.arange(total_rows, dtype=jnp.int32), TIMES)
     live_mask = time_step[None, None, :] < live_counts[:, :, None]

time: 119 us -> 117 us (0.983)
  waiting for transfers between devices: 19 us -> 16.6 us
  other arithmetic: 43 us -> 44.3 us
    all_to_all x1 -> x0, waiting for transfers between devices: 3.74 us -> none  [on_device(): lax.all_to_all(outgoing, 'chan', split_axis=2, concat_axis=3, tiled=True)]
    all_to_all x1 -> x0, starting transfers between devices: 3.25 us -> none  [on_device(): lax.all_to_all(outgoing, 'chan', split_axis=2, concat_axis=3, tiled=True)]
    ppermute x0 -> x3, starting transfers between devices: none -> 2.96 us  [on_device(): lax.ppermute(sent, 'chan', [(i, (i + hop) % size) for i in range(size)])]
    ppermute x0 -> x3, waiting for transfers between devices: none -> 1.32 us  [on_device(): lax.ppermute(sent, 'chan', [(i, (i + hop) % size) for i in range(size)])]
    another operation x1 -> x2, other arithmetic: 35.5 us -> 35.5 us
  transfers between devices with their start and end apart: 3 -> 5, of which waited for: 2 -> 4; matrix products, arithmetic and copies ran while one was open for 38% -> 39% of each run, Pallas kernels for 0% -> 0%
where the time goes in v1:
time: 117 us
  other arithmetic  44.3 us (38%)
  matrix products  33.8 us (29%)
  waiting for transfers between devices  16.6 us (14%)
  between operations  13.7 us (12%)
  local copies, waits for them, and re-layouts  5.5 us (5%)
  starting transfers between devices  3 us (3%)
    another operation x1, other arithmetic  35.5 us
    dot_general x4, matrix products, narrow_mix(): return jnp.einsum(pattern, left, right, preferred_element_type=jnp.float32)  16.4 us
    reduce_scatter x1, waiting for transfers between devices, on_device(): lax.psum_scatter(group_cuts, 'tile', scatter_dimension=0, tiled=True)  14.5 us
    dot_general x12, matrix products, exact_mix(): return jnp.einsum(pattern, left, right, precision=lax.Precision.HIGHEST)  11.4 us
    another operation x1, other arithmetic, tile_cuts(): jnp.stack([ev_real, ev_imag], axis=1).reshape(columns, 2 * block_size * SG)  6.18 us
    dot_general x1, matrix products, tile_cuts(): jnp.dot(strip_rows, phase_table, preferred_element_type=jnp.float32)  6 us
    ppermute x3, starting transfers between devices, on_device(): lax.ppermute(sent, 'chan', [(i, (i + hop) % size) for i in range(size)])  2.96 us
  transfers between devices with their start and end apart: 5, of which 4 were waited for; matrix products, arithmetic and copies ran while one was open for 39% of the time, Pallas kernels for 0%

profile of v1, /device:TPU:0, one launch (start us, length us, event | category | flops | bytes accessed | tf_op | source)
XLA Modules:
  0.0 116.8 jit_solution(2856119999899609567)
XLA Ops:
  6.5 0.0 all-gather.2.cloned.1.call-start
  6.5 0.7 all-gather.2.cloned.1.call-update
  7.3 0.0 reduce-scatter.2.cloned.1.call-start
  7.3 0.8 fusion.81
  8.1 0.1 iota_add_fusion
  8.2 0.1 iota_add_fusion.1
  8.3 0.1 add_add_fusion
  8.3 0.8 fusion.83
  9.1 0.7 gather_fusion
  9.9 0.7 gather_fusion.1
  10.6 0.7 broadcast_compare_fusion
  11.4 0.1 sub.80
  11.5 0.1 add.291
  11.6 0.1 sub.90
  11.7 35.5 %cosine_convert_fusion = (bf16[2048,1,32,32]{0,3,2,1:T(8,128)(2,1)S(1)}, bf16[2048,1,32,32]{0,3,2,1:T(8,128)(2,1)}) fusion(s32[32,32]{1,0:T(8,128)S(1)} %iota_add_fusion, s32[2048]{0:T(1024)S(1)} %iota_add_fusion.2), kind=kLoop, calls=%fused_computation.13 | loop fusion | flops 35651584 | bytes 8400896 | tf_op jit(solution)/shard_map/convert
  47.2 6.2 %pad_maximum_fusion = bf16[2048,2,32,32]{0,3,2,1:T(8,128)(2,1)} fusion(bf16[2048,1,32,32]{0,3,2,1:T(8,128)(2,1)} %get-tuple-element.31, bf16[2048,1,32,32]{0,3,2,1:T(8,128)(2,1)S(1)} %get-tuple-element.30), kind=kLoop, calls=%fused_computation.11 | loop fusion | flops 4194304 | bytes 16777216 | tf_op jit(solution)/shard_map/while/body/eval_jaxpr/stack | solution.py:48
  53.4 6.0 %convolution_convert_fusion = bf16[2048,256]{1,0:T(8,128)(2,1)S(1)} fusion(bf16[2048,2048]{0,1:T(8,128)(2,1)} %bitcast.105, bf16[256,2048]{1,0:T(8,128)(2,1)} %bitcast.120), kind=kOutput, calls=%fused_computation.14 | convolution fusion | flops 2148007936 | bytes 10485760 | tf_op jit(solution)/shard_map/while/body/eval_jaxpr/dot_general | solution.py:52
  59.4 4.0 %fusion.15 = f32[32,32,32]{2,1,0:T(8,128)S(1)} fusion(s32[256]{0:T(256)S(1)} %sub.80, s32[32,32]{1,0:T(8,128)S(1)} %iota_add_fusion.1, bf16[256,2,32,32]{0,3,2,1:T(8,128)(2,1)S(1)} %bitcast.121), kind=kOutput, calls=%fused_computation.45 | convolution fusion | flops 20709376 | bytes 672768 | tf_op jit(solution)/shard_map/while/body/eval_jaxpr/jal,ljb->jab/dot_general | solution.py:33
  63.4 4.0 %fusion.14 = f32[32,32,32]{2,1,0:T(8,128)S(1)} fusion(s32[256]{0:T(256)S(1)} %sub.80, s32[32,32]{1,0:T(8,128)S(1)} %iota_add_fusion.1, bf16[256,2,32,32]{0,3,2,1:T(8,128)(2,1)S(1)} %bitcast.122), kind=kOutput, calls=%fused_computation.44 | convolution fusion | flops 20709376 | bytes 672768 | tf_op jit(solution)/shard_map/while/body/eval_jaxpr/jal,ljb->jab/dot_general | solution.py:33
  67.4 4.3 %fusion.4 = f32[32,1,32,32]{3,2,0,1:T(8,128)S(1)} fusion(f32[32,32,32]{2,1,0:T(8,128)S(1)} %fusion.15, s32[256]{0:T(256)S(1)} %sub.80, s32[32,32]{1,0:T(8,128)S(1)} %iota_add_fusion.1, bf16[256,2,32,32]{0,3,2,1:T(8,128)(2,1)S(1)} %bitcast.123), kind=kOutput, calls=%fused_computation.23 | convolution fusion | flops 21004288 | bytes 1197056 | tf_op jit(solution)/shard_map/while/body/eval_jaxpr/jal,ljb->jab/dot_general | solution.py:33
  71.7 4.1 %fusion.3 = f32[32,1,32,32]{3,2,0,1:T(8,128)S(1)} fusion(f32[32,32,32]{2,1,0:T(8,128)S(1)} %fusion.14, s32[256]{0:T(256)S(1)} %sub.80, s32[32,32]{1,0:T(8,128)S(1)} %iota_add_fusion.1, bf16[256,2,32,32]{0,3,2,1:T(8,128)(2,1)S(1)} %bitcast.124), kind=kOutput, calls=%fused_computation.21 | convolution fusion | flops 21004288 | bytes 1197056 | tf_op jit(solution)/shard_map/while/body/eval_jaxpr/jal,ljb->jab/dot_general | solution.py:33
  75.8 0.1 pad_maximum_fusion.1
  75.9 0.1 copy.19
  76.0 1.2 %reshape.333 = f32[32,2048]{1,0:T(8,128)} reshape(f32[32,2,32,32]{3,2,1,0:T(8,128)S(1)} %copy.19) | data formatting | bytes 524288 | tf_op jit(solution)/shard_map/reshape | solution.py:79
  77.2 0.0 reduce-scatter.2.cloned.1.call-update
  77.2 0.1 broadcast_multiply_fusion
  77.3 14.5 %reduce-scatter.2.cloned.1.call-done = f32[16,2048]{1,0:T(8,128)} async-done(((f32[32,2048]{1,0:T(8,128)}), f32[16,2048]{1,0:T(8,128)}) %reduce-scatter.2.cloned.1.call-update) | async-done | bytes 131088 | tf_op jit(solution)/shard_map/reduce_scatter | solution.py:155
  91.8 1.1 reshape.334
  92.9 0.6 fusion.23
  93.5 0.6 fusion.22
  94.1 0.6 fusion.10
  94.7 0.6 fusion.46
  95.3 0.6 fusion.39
  95.9 0.6 fusion.9
  96.5 0.9 fusion.8
  97.4 0.6 multiply_add_fusion
  98.0 1.3 %fusion.20 = f32[16,32,128]{2,1,0:T(8,128)S(1)} fusion(f32[16,32,32]{2,1,0:T(8,128)S(1)} %get-tuple-element.27, f32[16,128]{1,0:T(8,128)S(1)} %get-tuple-element.37, f32[32]{0:T(128)S(1)} %iota_convert_fusion), kind=kOutput, calls=%fused_computation.58 | convolution fusion | flops 25362432 | bytes 336000 | tf_op jit(solution)/shard_map/jxy,jky->jxk/dot_general | solution.py:37
  99.3 1.3 %fusion.18 = f32[16,32,128]{2,1,0:T(8,128)S(1)} fusion(f32[16,32,32]{2,1,0:T(8,128)S(1)} %get-tuple-element.27, f32[16,128]{1,0:T(8,128)S(1)} %get-tuple-element.37, f32[32]{0:T(128)S(1)} %iota_convert_fusion), kind=kOutput, calls=%fused_computation.57 | convolution fusion | flops 25296896 | bytes 336000 | tf_op jit(solution)/shard_map/jxy,jky->jxk/dot_general | solution.py:37
  100.6 1.3 %fusion.5 = f32[16,128,32]{1,2,0:T(8,128)S(1)} fusion(f32[16,32,128]{2,1,0:T(8,128)S(1)} %fusion.20, f32[16,32,32]{2,1,0:T(8,128)S(1)} %get-tuple-element.26, f32[16,128]{1,0:T(8,128)S(1)} %get-tuple-element.37, f32[32]{0:T(128)S(1)} %iota_convert_fusion), kind=kOutput, calls=%fused_computation.25 | convolution fusion | flops 25362432 | bytes 598144 | tf_op jit(solution)/shard_map/jxy,jky->jxk/dot_general | solution.py:37
  102.0 2.4 %multiply_reduce_fusion = (f32[16,128]{1,0:T(8,128)S(1)}, f32[16,128]{1,0:T(8,128)S(1)}, f32[16,128]{1,0:T(8,128)S(1)}, f32[16,128]{1,0:T(8,128)S(1)}) fusion(f32[32]{0:T(128)S(1)} %iota_convert_fusion, f32[16,128]{1,0:T(8,128)S(1)} %get-tuple-element.36, f32[16,128,32]{1,2,0:T(8,128)S(1)} %fusion.5, f32[16,32,128]{2,1,0:T(8,128)S(1)} %fusion.18, ...), kind=kOutput, calls=%fused_computation.48 | convolution fusion | flops 26140672 | bytes 639104 | tf_op jit(solution)/shard_map/jxy,jky->jxk/dot_general | solution.py:37
  104.4 0.1 collective-permute-start
  104.5 1.5 %collective-permute-start.1 = (f32[2,4,1,128]{3,1,0,2:T(4,128)S(1)}, f32[2,4,1,128]{3,1,0,2:T(4,128)S(1)}, u32[]{:S(2)}, u32[]{:S(2)}) collective-permute-start(f32[2,4,1,128]{3,1,0,2:T(4,128)S(1)} %bitcast.114), channel_id=1, source_target_pairs={{0,4},{2,6},{4,0},{6,2},{1,5},{3,7},{5,1},{7,3},{8,12},{10,14},{12... | collective-permute-start | bytes 12296 | tf_op jit(solution)/shard_map/ppermute | solution.py:164
  106.0 1.4 %collective-permute-start.2 = (f32[2,4,1,128]{3,1,0,2:T(4,128)S(1)}, f32[2,4,1,128]{3,1,0,2:T(4,128)S(1)}, u32[]{:S(2)}, u32[]{:S(2)}) collective-permute-start(f32[2,4,1,128]{3,1,0,2:T(4,128)S(1)} %bitcast.113), channel_id=1, source_target_pairs={{0,6},{2,0},{4,2},{6,4},{1,7},{3,1},{5,3},{7,5},{8,14},{10,8},{12,... | collective-permute-start | bytes 12296 | tf_op jit(solution)/shard_map/ppermute | solution.py:164
  107.4 0.1 collective-permute-done
  107.5 0.7 collective-permute-done.1
  108.2 0.6 collective-permute-done.2
  108.7 0.6 gather_fusion.2
  109.3 0.6 broadcast_select_fusion
  (23 shorter events, 0.1 us)
Async XLA Ops:
  6.5 2.6 %copy-start = (f32[2,64,1024]{2,1,0:T(8,128)S(1)}, f32[2,64,1024]{2,1,0:T(8,128)}, u32[]{:S(2)}) copy-start(f32[2,64,1024]{2,1,0:T(8,128)} %param.8) | copy-start | bytes 1572868
  6.5 46.8 %all-gather.2.cloned.1.call-start = ((), (), s32[]{:S(2)}) async-start(), calls=%async_computation.1 | async-start | bytes 1310720 | tf_op jit(solution)/shard_map/all_gather | solution.py:148
  7.3 84.6 %reduce-scatter.2.cloned.1.call-start = ((), (), s32[]{:S(2)}) async-start(), calls=%async_computation.2 | async-start | bytes 393216 | tf_op jit(solution)/shard_map/reduce_scatter | solution.py:155
  67.4 9.9 %copy-start.2 = (f32[2,16,128]{2,1,0:T(8,128)S(1)}, f32[2,16,128]{2,1,0:T(8,128)}, u32[]{:S(2)}) copy-start(f32[2,16,128]{2,1,0:T(8,128)} %param.11) | copy-start | bytes 49156
  75.8 33.6 %copy-start.1 = (f32[2,4,1,512]{3,2,1,0:T(1,128)S(1)}, f32[2,4,1,512]{3,2,1,0:T(1,128)}, u32[]{:S(2)}) copy-start(f32[2,4,1,512]{3,2,1,0:T(1,128)} %param.12) | copy-start | bytes 49156
  104.4 3.1 %collective-permute-start = (f32[2,4,1,128]{3,1,0,2:T(4,128)S(1)}, f32[2,4,1,128]{3,1,0,2:T(4,128)S(1)}, u32[]{:S(2)}, u32[]{:S(2)}) collective-permute-start(f32[2,4,1,128]{3,1,0,2:T(4,128)S(1)} %bitcast.115), channel_id=1, source_target_pairs={{0,2},{2,4},{4,6},{6,0},{1,3},{3,5},{5,7},{7,1},{8,10},{10,12},{12... | collective-permute-start | bytes 12296 | tf_op jit(solution)/shard_map/ppermute | solution.py:164
  104.5 3.7 %collective-permute-start.1 = (f32[2,4,1,128]{3,1,0,2:T(4,128)S(1)}, f32[2,4,1,128]{3,1,0,2:T(4,128)S(1)}, u32[]{:S(2)}, u32[]{:S(2)}) collective-permute-start(f32[2,4,1,128]{3,1,0,2:T(4,128)S(1)} %bitcast.114), channel_id=1, source_target_pairs={{0,4},{2,6},{4,0},{6,2},{1,5},{3,7},{5,1},{7,3},{8,12},{10,14},{12... | collective-permute-start | bytes 12296 | tf_op jit(solution)/shard_map/ppermute | solution.py:164
  106.0 2.7 %collective-permute-start.2 = (f32[2,4,1,128]{3,1,0,2:T(4,128)S(1)}, f32[2,4,1,128]{3,1,0,2:T(4,128)S(1)}, u32[]{:S(2)}, u32[]{:S(2)}) collective-permute-start(f32[2,4,1,128]{3,1,0,2:T(4,128)S(1)} %bitcast.113), channel_id=1, source_target_pairs={{0,6},{2,0},{4,2},{6,4},{1,7},{3,1},{5,3},{7,5},{8,14},{10,8},{12,... | collective-permute-start | bytes 12296 | tf_op jit(solution)/shard_map/ppermute | solution.py:164
Sparse Core Ops, SparseCore 0:
  8.9 30.8 all-gather.1
  77.3 14.4 reduce-scatter.1
